TPU v7x, 32 devices: a whole 2x2x4 slice. The times are simulated.
32 devices in a mesh: row: 4 (over z), col: 8 (over y, x, core).
Axes of the slice: x: 2, y: 2, z: 4, core: 2. Of those that a mesh axis runs over, the one named last changes fastest.
Arguments:
- pair: bfloat16 [256, 256, 128], P('row', 'col'), may hold values from -6 to 6
- mask: int32 [256], replicated, may hold values from 0 to 1, as said below
- chain: int32 [256], replicated, may hold values from 0 to 3, never falling along the last dimension, each value on 1 to 128 neighbouring positions
- w_ap: bfloat16 [128, 128], replicated, may hold values from -0.5 to 0.5
- w_ag: bfloat16 [128, 128], replicated, may hold values from -0.5 to 0.5
- w_bp: bfloat16 [128, 128], replicated, may hold values from -0.5 to 0.5
- w_bg: bfloat16 [128, 128], replicated, may hold values from -0.5 to 0.5
- w_gate: bfloat16 [128, 128], replicated, may hold values from -0.5 to 0.5
- w_out: bfloat16 [128, 128], replicated, may hold values from -0.5 to 0.5
- chain_bias: float32 [128], replicated, may hold values from -4 to 4
Outputs:
- update: bfloat16 [256, 256, 128], P('row', 'col')
Inputs may be any that keep to these rules, and one draw needn't show every extreme that they name: `mask`: tokens from some position between 128 and 256 on are all padding (0); before it about one token in sixteen is 0 too.
All inputs are finite; a program needn't handle non-finite values.
Results may differ from a plain program's by a relative error of at most 0.012.
Values may be sent and summed in bfloat16 or wider, within the bound.
A program may use at most 64 MiB of HBM per device.

v0:
```python
import jax
import jax.numpy as jnp
from jax import lax
from jax.sharding import PartitionSpec as P


def channel_norm(values, axis):
    mean = jnp.mean(values, axis=axis, keepdims=True)
    centred = values - mean
    spread = jnp.mean(centred * centred, axis=axis, keepdims=True)
    return centred * lax.rsqrt(spread + 1e-05)


def shards(pair, mask, chain, w_ap, w_ag, w_bp, w_bg, w_gate, w_out, chain_bias):
    tok_i, tok_j, width = pair.shape
    hidden = w_ap.shape[1]
    row_index = lax.axis_index("row")
    col_index = lax.axis_index("col")
    row_start = row_index * tok_i
    col_start = col_index * tok_j
    mask_f = mask.astype(jnp.float32)
    mask_rows = lax.dynamic_slice_in_dim(mask_f, row_start, tok_i, 0)
    mask_cols = lax.dynamic_slice_in_dim(mask_f, col_start, tok_j, 0)
    zn = channel_norm(pair.astype(jnp.float32), -1).astype(jnp.bfloat16)
    flat = zn.reshape(tok_i * tok_j, width)
    stacked = jnp.concatenate([w_ap, w_ag, w_bp, w_bg], axis=1)
    projected = jnp.dot(flat, stacked, preferred_element_type=jnp.float32)
    pair_mask = (mask_rows[:, None] * mask_cols[None, :]).reshape(tok_i * tok_j, 1)
    left_p = projected[:, 0:hidden]
    left_g = projected[:, hidden : 2 * hidden]
    right_p = projected[:, 2 * hidden : 3 * hidden]
    right_g = projected[:, 3 * hidden : 4 * hidden]
    left_own = (pair_mask * jax.nn.sigmoid(left_g) * left_p).astype(jnp.bfloat16)
    right_own = (pair_mask * jax.nn.sigmoid(right_g) * right_p).astype(jnp.bfloat16)
    left_t = left_own.reshape(tok_i, tok_j, hidden).transpose(2, 0, 1)
    right_t = right_own.reshape(tok_i, tok_j, hidden).transpose(2, 0, 1)
    left_c, right_c = (
        lax.all_to_all(left_t, "col", split_axis=0, concat_axis=2, tiled=True),
        lax.all_to_all(right_t, "col", split_axis=0, concat_axis=2, tiled=True),
    )
    left_k = lax.all_to_all(left_c, "row", split_axis=2, concat_axis=1, tiled=True)
    partial_value = jnp.einsum(
        "cki,ckj->cij",
        left_k,
        lax.all_gather(right_c, "row", axis=1, tiled=True),
        preferred_element_type=jnp.float32,
    )
    mixed = lax.all_to_all(
        partial_value.astype(jnp.bfloat16), "col", split_axis=2, concat_axis=0, tiled=True
    ).astype(partial_value.dtype)
    normed = channel_norm(mixed, 0).astype(jnp.bfloat16).reshape(hidden, tok_i * tok_j)
    output = jnp.einsum("cp,cd->pd", normed, w_out, preferred_element_type=jnp.float32)
    chain_rows = lax.dynamic_slice_in_dim(chain, row_start, tok_i, 0)
    chain_cols = lax.dynamic_slice_in_dim(chain, col_start, tok_j, 0)
    same = (
        (chain_rows[:, None] == chain_cols[None, :]).astype(jnp.float32).reshape(tok_i * tok_j, 1)
    )
    gate = jnp.dot(flat, w_gate, preferred_element_type=jnp.float32) + same * chain_bias[None, :]
    update = (jax.nn.sigmoid(gate) * output).astype(jnp.bfloat16)
    return update.reshape(tok_i, tok_j, width)


def solution(mesh):
    return jax.shard_map(
        shards,
        mesh=mesh,
        in_specs=(P("row", "col", None), P(), P(), P(), P(), P(), P(), P(), P(), P()),
        out_specs=P("row", "col", None),
        check_vma=False,
    )
```

profile of v0, /device:TPU:0, one launch (start us, length us, event | category | flops | bytes accessed | tf_op | source)
XLA Modules:
  0.0 125.9 jit_solution(9801597278587520292)
XLA Ops:
  6.5 0.0 copy-start
  6.5 0.0 all-gather.2.cloned.1.call-start
  6.6 0.7 convert_element_type.58
  7.3 0.1 dynamic_slice.14
  7.4 0.1 dynamic_slice.15
  7.4 0.1 broadcast_multiply_fusion
  7.5 0.1 mul.97
  7.6 1.4 %convert_reduce_fusion = f32[64,32]{1,0:T(8,128)S(1)} fusion(bf16[64,32,128]{2,1,0:T(8,128)(2,1)} %param.10), kind=kLoop, calls=%fused_computation.10 | loop fusion | flops 522240 | bytes 532480 | tf_op jit(solution)/shard_map/reduce_sum | solution.py:8
  9.0 1.7 %fusion.7 = f32[64,32]{1,0:T(8,128)S(1)} fusion(bf16[64,32,128]{2,1,0:T(8,128)(2,1)} %param.10, f32[64,32]{1,0:T(8,128)S(1)} %broadcast_multiply_fusion.2), kind=kLoop, calls=%fused_computation.14 | loop fusion | flops 1046528 | bytes 540672 | tf_op jit(solution)/shard_map/reduce_sum | solution.py:10
  10.7 1.6 %fusion.8 = bf16[64,32,128]{2,1,0:T(8,128)(2,1)S(1)} fusion(bf16[64,32,128]{2,1,0:T(8,128)(2,1)} %param.10, f32[64,32]{1,0:T(8,128)S(1)} %add_rsqrt_fusion.1, f32[64,32]{1,0:T(8,128)S(1)} %broadcast_multiply_fusion.2), kind=kLoop, calls=%fused_computation.15 | loop fusion | flops 1048576 | bytes 1064960 | tf_op jit(solution)/shard_map/convert_element_type | solution.py:24
  12.3 0.0 copy-done.5
  12.4 0.0 copy-done.4
  12.4 0.0 copy-done.3
  12.4 0.0 copy-done.2
  12.4 0.7 fusion.22
  13.1 0.6 fusion.10
  13.7 1.7 %copy.42 = bf16[64,32,128]{0,1,2:T(8,128)(2,1)S(1)} copy(bf16[64,32,128]{2,1,0:T(8,128)(2,1)S(1)} %bitcast.64) | data formatting | bytes 1048576 | tf_op jit(solution)/shard_map/reshape | solution.py:36
  15.4 0.1 bitcast_bitcast_fusion
  15.4 0.7 reshape.107
  16.2 14.7 %all_to_all.63 = bf16[8,2,16384]{2,1,0:T(2,128)(2,1)S(1)} all-to-all(bf16[8,2,16384]{2,1,0:T(2,128)(2,1)S(1)} %reshape.107), channel_id=1, replica_groups=mesh['row'=4,'col'=8] {'col'}, dimensions={0} | all-to-all | bytes 1048576 | tf_op jit(solution)/shard_map/all_to_all | solution.py:39
  30.9 0.7 reshape.108
  31.5 0.1 copy.43
  31.6 1.1 copy.44
  32.8 0.0 all-gather.2.cloned.1.call-update
  32.8 1.7 %copy.37 = bf16[64,32,128]{0,1,2:T(8,128)(2,1)S(1)} copy(bf16[64,32,128]{2,1,0:T(8,128)(2,1)S(1)} %bitcast.63) | data formatting | bytes 1048576 | tf_op jit(solution)/shard_map/reshape | solution.py:35
  34.5 0.1 bitcast_bitcast_fusion.1
  34.6 0.7 reshape.103
  35.3 12.1 %all_to_all.64 = bf16[8,2,16384]{2,1,0:T(2,128)(2,1)S(1)} all-to-all(bf16[8,2,16384]{2,1,0:T(2,128)(2,1)S(1)} %reshape.103), channel_id=1, replica_groups=mesh['row'=4,'col'=8] {'col'}, dimensions={0} | all-to-all | bytes 1048576 | tf_op jit(solution)/shard_map/all_to_all | solution.py:38
  47.4 0.7 reshape.104
  48.1 0.1 copy.38
  48.2 0.0 copy-start.7
  48.2 0.7 copy.58
  48.9 1.6 %reshape.105 = bf16[4,2,32768]{2,1,0:T(2,128)(2,1)} reshape(bf16[256,16,64]{2,1,0:T(8,128)(2,1)S(1)} %bitcast.59) | data formatting | bytes 1048576
  50.4 4.9 %all-to-all-start.1 = ((bf16[4,2,32768]{2,1,0:T(2,128)(2,1)}), bf16[4,2,32768]{2,1,0:T(2,128)(2,1)S(1)}, u32[]{:S(2)}, u32[]{:S(2)}) async-start(bf16[4,2,32768]{2,1,0:T(2,128)(2,1)} %reshape.105), calls=%async_computation.1 | async-start | bytes 1048576 | tf_op jit(solution)/shard_map/all_to_all | solution.py:41
  55.3 0.0 copy-done.7
  55.3 0.1 dynamic_slice.12
  55.4 0.1 dynamic_slice.13
  55.5 28.6 %all-to-all-done.1 = bf16[4,2,32768]{2,1,0:T(2,128)(2,1)S(1)} async-done(((bf16[4,2,32768]{2,1,0:T(2,128)(2,1)}), bf16[4,2,32768]{2,1,0:T(2,128)(2,1)S(1)}, u32[]{:S(2)}, u32[]{:S(2)}) %all-to-all-start.1) | async-done | bytes 524320 | tf_op jit(solution)/shard_map/all_to_all | solution.py:41
  84.1 0.7 reshape.106
  84.8 0.8 copy.57
  85.6 0.7 all_to_all.53
  86.3 2.9 %all-gather.2.cloned.1.call-done = bf16[16,256,256]{2,1,0:T(8,128)(2,1)} async-done(((bf16[16,64,256]{2,1,0:T(8,128)(2,1)}), bf16[16,256,256]{2,1,0:T(8,128)(2,1)}) %all-gather.2.cloned.1.call-update) | async-done | bytes 2097168 | tf_op jit(solution)/shard_map/all_gather | solution.py:45
  89.2 2.1 %convolution_convert_fusion = bf16[16,64,256]{2,1,0:T(8,128)(2,1)S(1)} fusion(bf16[16,256,64]{1,2,0:T(8,128)(2,1)S(1)} %all_to_all.53, bf16[16,256,256]{2,1,0:T(8,128)(2,1)} %all-gather.2.cloned.1.call-done), kind=kOutput, calls=%fused_computation.11 | convolution fusion | flops 134479872 | bytes 3145728 | tf_op jit(solution)/shard_map/cki,ckj->cij/dot_general | solution.py:42
  91.3 0.0 copy-start.8
  91.3 1.0 copy.45
  92.3 1.5 %reshape.109 = bf16[8,2,16384]{2,1,0:T(2,128)(2,1)} reshape(bf16[256,16,64]{2,1,0:T(8,128)(2,1)S(1)} %bitcast.54) | data formatting | bytes 1048576
  93.8 3.7 %all-to-all-start.3 = ((bf16[8,2,16384]{2,1,0:T(2,128)(2,1)}), bf16[8,2,16384]{2,1,0:T(2,128)(2,1)S(1)}, u32[]{:S(2)}, u32[]{:S(2)}) async-start(bf16[8,2,16384]{2,1,0:T(2,128)(2,1)} %reshape.109), calls=%async_computation.3 | async-start | bytes 1048576 | tf_op jit(solution)/shard_map/all_to_all | solution.py:48
  97.4 0.1 compare_convert_fusion
  97.5 0.1 reshape.99
  97.6 0.0 copy-done
  97.6 1.4 %fusion.3 = f32[2048,128]{1,0:T(8,128)} fusion(bf16[2048,128]{1,0:T(8,128)(2,1)S(1)} %bitcast.66, bf16[128,128]{1,0:T(8,128)(2,1)S(1)} %copy-done, f32[128]{0:T(128)S(1)} %copy-done.8, f32[2048]{0:T(1024)S(1)} %reshape.99), kind=kOutput, calls=%fused_computation.5 | convolution fusion | flops 68419584 | bytes 1614336 | tf_op jit(solution)/shard_map/dot_general | solution.py:58
  99.0 8.1 %all-to-all-done.3 = bf16[8,2,16384]{2,1,0:T(2,128)(2,1)S(1)} async-done(((bf16[8,2,16384]{2,1,0:T(2,128)(2,1)}), bf16[8,2,16384]{2,1,0:T(2,128)(2,1)S(1)}, u32[]{:S(2)}, u32[]{:S(2)}) %all-to-all-start.3) | async-done | bytes 524320 | tf_op jit(solution)/shard_map/all_to_all | solution.py:48
  107.1 1.6 %reshape.110 = bf16[256,16,64]{2,1,0:T(8,128)(2,1)} reshape(bf16[8,2,16384]{2,1,0:T(2,128)(2,1)S(1)} %all-to-all-done.3) | data formatting | bytes 1048576
  108.8 1.6 %fusion.31 = (bf16[16,64,256]{1,2,0:T(8,128)(2,1)S(1)}, f32[8,16,64,32]{2,3,0,1:T(8,128)S(1)}) fusion(bf16[16,64,256]{1,0,2:T(8,128)(2,1)} %bitcast.62), kind=kLoop, calls=%fused_computation.50 | loop fusion | flops 262144 | bytes 2097152 | tf_op jit(solution)/shard_map/all_to_all | solution.py:48
  110.3 0.3 fusion.9
  110.6 0.1 copy.48
  110.7 0.1 copy.49
  110.8 0.1 div.29
  110.8 0.4 multiply_reduce_fusion
  111.2 0.1 copy.50
  111.3 0.1 rsqrt.21
  111.4 2.7 %copy.47 = f32[8,16,64,32]{3,2,1,0:T(8,128)} copy(f32[8,16,64,32]{2,3,0,1:T(8,128)S(1)} %get-tuple-element.8) | data formatting | bytes 2097152 | tf_op jit(solution)/shard_map/convert_element_type | solution.py:50
  114.1 3.7 %reshape.100 = f32[128,2048]{1,0:T(8,128)S(1)} reshape(f32[8,16,64,32]{3,2,1,0:T(8,128)} %copy.47) | data formatting | bytes 2097152 | tf_op jit(solution)/shard_map/convert_element_type | solution.py:50
  117.9 1.1 fusion.4
  (13 shorter events, 0.1 us)
Async XLA Ops:
  6.5 91.0 %copy-start = (bf16[128,128]{1,0:T(8,128)(2,1)S(1)}, bf16[128,128]{1,0:T(8,128)(2,1)}, u32[]{:S(2)}) copy-start(bf16[128,128]{1,0:T(8,128)(2,1)} %param.17) | copy-start | bytes 98308
  6.5 5.8 %copy-start.5 = (bf16[128,128]{1,0:T(8,128)(2,1)S(1)}, bf16[128,128]{1,0:T(8,128)(2,1)}, u32[]{:S(2)}) copy-start(bf16[128,128]{1,0:T(8,128)(2,1)} %param.13) | copy-start | bytes 98308
  6.5 5.8 %copy-start.4 = (bf16[128,128]{1,0:T(8,128)(2,1)S(1)}, bf16[128,128]{1,0:T(8,128)(2,1)}, u32[]{:S(2)}) copy-start(bf16[128,128]{1,0:T(8,128)(2,1)} %param.14) | copy-start | bytes 98308
  6.5 5.8 %copy-start.3 = (bf16[128,128]{1,0:T(8,128)(2,1)S(1)}, bf16[128,128]{1,0:T(8,128)(2,1)}, u32[]{:S(2)}) copy-start(bf16[128,128]{1,0:T(8,128)(2,1)} %param.15) | copy-start | bytes 98308
  6.5 5.8 %copy-start.2 = (bf16[128,128]{1,0:T(8,128)(2,1)S(1)}, bf16[128,128]{1,0:T(8,128)(2,1)}, u32[]{:S(2)}) copy-start(bf16[128,128]{1,0:T(8,128)(2,1)} %param.16) | copy-start | bytes 98308
  6.5 82.7 %all-gather.2.cloned.1.call-start = ((), (), s32[]{:S(2)}) async-start(), calls=%async_computation.4 | async-start | bytes 2621440 | tf_op jit(solution)/shard_map/all_gather | solution.py:45
  48.2 7.1 %copy-start.7 = (s32[256]{0:T(256)S(1)}, s32[256]{0:T(256)}, u32[]{:S(2)}) copy-start(s32[256]{0:T(256)} %param.12) | copy-start | bytes 3076
  50.4 33.6 %all-to-all-start.1 = ((bf16[4,2,32768]{2,1,0:T(2,128)(2,1)}), bf16[4,2,32768]{2,1,0:T(2,128)(2,1)S(1)}, u32[]{:S(2)}, u32[]{:S(2)}) async-start(bf16[4,2,32768]{2,1,0:T(2,128)(2,1)} %reshape.105), calls=%async_computation.1 | async-start | bytes 1048576 | tf_op jit(solution)/shard_map/all_to_all | solution.py:41
  91.3 6.3 %copy-start.8 = (f32[128]{0:T(128)S(1)}, f32[128]{0:T(128)}, u32[]{:S(2)}) copy-start(f32[128]{0:T(128)} %param.19) | copy-start | bytes 1540
  93.8 13.4 %all-to-all-start.3 = ((bf16[8,2,16384]{2,1,0:T(2,128)(2,1)}), bf16[8,2,16384]{2,1,0:T(2,128)(2,1)S(1)}, u32[]{:S(2)}, u32[]{:S(2)}) async-start(bf16[8,2,16384]{2,1,0:T(2,128)(2,1)} %reshape.109), calls=%async_computation.3 | async-start | bytes 1048576 | tf_op jit(solution)/shard_map/all_to_all | solution.py:48
  114.1 3.7 %copy-start.1 = (f32[2048,128]{1,0:T(8,128)S(1)}, f32[2048,128]{1,0:T(8,128)}, u32[]{:S(2)}) copy-start(f32[2048,128]{1,0:T(8,128)} %fusion.3) | copy-start | bytes 3145732
  114.1 3.8 %copy-start.6 = (bf16[128,128]{1,0:T(8,128)(2,1)S(1)}, bf16[128,128]{1,0:T(8,128)(2,1)}, u32[]{:S(2)}) copy-start(bf16[128,128]{1,0:T(8,128)(2,1)} %param.18) | copy-start | bytes 98308
Sparse Core Ops, SparseCore 0:
  32.9 56.2 all-gather.1
where the time goes:
time: 127 us; the launch traced here: 126 us
  waiting for transfers between devices  39.7 us (31%)
  blocking collectives  26.8 us (21%)
  local copies, waits for them, and re-layouts  23.4 us (18%)
  between operations  13.7 us (11%)
  starting transfers between devices  8.57 us (7%)
  other arithmetic  8.37 us (7%)
  matrix products  5.31 us (4%)
    all_to_all x1, waiting for transfers between devices, shards(): lax.all_to_all(left_c, 'row', split_axis=2, concat_axis=1, tiled=True)  28.6 us
    all_to_all x1, blocking collectives, shards(): lax.all_to_all(right_t, 'col', split_axis=0, concat_axis=2, tiled=True)  14.7 us
    all_to_all x1, blocking collectives, shards(): lax.all_to_all(left_t, 'col', split_axis=0, concat_axis=2, tiled=True)  12.1 us
    unnamed x28, local copies, waits for them, and re-layouts  8.29 us
    all_to_all x1, waiting for transfers between devices, shards(): lax.all_to_all(partial_value.astype(jnp.bfloat16), 'col', split_axis=2, c...  8.14 us
    convert_element_type x2, local copies, waits for them, and re-layouts, shards(): mixed = lax.all_to_all(partial_value.astype(jnp.bfloat16), 'col', split_a...  6.46 us
    all_to_all x1, starting transfers between devices, shards(): lax.all_to_all(left_c, 'row', split_axis=2, concat_axis=1, tiled=True)  4.87 us
    all_to_all x1, starting transfers between devices, shards(): lax.all_to_all(partial_value.astype(jnp.bfloat16), 'col', split_axis=2, c...  3.66 us
  transfers between devices with their start and end apart: 3, of which 3 were waited for; matrix products, arithmetic and copies ran while one was open for 7% of the time, Pallas kernels for 0%

commit v1 on v0

--- a/solution.py
+++ b/solution.py
@@ -32,23 +32,21 @@
     right_g = projected[:, 3 * hidden : 4 * hidden]
     left_own = (pair_mask * jax.nn.sigmoid(left_g) * left_p).astype(jnp.bfloat16)
     right_own = (pair_mask * jax.nn.sigmoid(right_g) * right_p).astype(jnp.bfloat16)
-    left_t = left_own.reshape(tok_i, tok_j, hidden).transpose(2, 0, 1)
-    right_t = right_own.reshape(tok_i, tok_j, hidden).transpose(2, 0, 1)
-    left_c, right_c = (
-        lax.all_to_all(left_t, "col", split_axis=0, concat_axis=2, tiled=True),
-        lax.all_to_all(right_t, "col", split_axis=0, concat_axis=2, tiled=True),
-    )
-    left_k = lax.all_to_all(left_c, "row", split_axis=2, concat_axis=1, tiled=True)
-    partial_value = jnp.einsum(
-        "cki,ckj->cij",
-        left_k,
-        lax.all_gather(right_c, "row", axis=1, tiled=True),
-        preferred_element_type=jnp.float32,
-    )
-    mixed = lax.all_to_all(
-        partial_value.astype(jnp.bfloat16), "col", split_axis=2, concat_axis=0, tiled=True
-    ).astype(partial_value.dtype)
-    normed = channel_norm(mixed, 0).astype(jnp.bfloat16).reshape(hidden, tok_i * tok_j)
+    axes = ("row", "col")
+    n_row, n_col = lax.axis_size("row"), lax.axis_size("col")
+    n_dev = n_row * n_col
+    own = hidden // n_dev
+    both = jnp.stack([left_own, right_own]).reshape(2, tok_i * tok_j, n_dev, own)
+    both = both.transpose(2, 0, 3, 1)
+    both = lax.all_to_all(both, axes, split_axis=0, concat_axis=0, tiled=True)
+    both = both.reshape(n_row, n_col, 2, own, tok_i, tok_j).transpose(2, 3, 0, 4, 1, 5)
+    both = both.reshape(2, own, n_row * tok_i, n_col * tok_j)
+    product = jnp.einsum("cki,ckj->cij", both[0], both[1], preferred_element_type=jnp.float32)
+    product = product.astype(jnp.bfloat16).reshape(own, n_row, tok_i, n_col, tok_j)
+    product = product.transpose(1, 3, 0, 2, 4).reshape(n_dev, own, tok_i * tok_j)
+    mixed = lax.all_to_all(product, axes, split_axis=0, concat_axis=0, tiled=True)
+    mixed = mixed.reshape(hidden, tok_i * tok_j).astype(jnp.float32)
+    normed = channel_norm(mixed, 0).astype(jnp.bfloat16)
     output = jnp.einsum("cp,cd->pd", normed, w_out, preferred_element_type=jnp.float32)
     chain_rows = lax.dynamic_slice_in_dim(chain, row_start, tok_i, 0)
     chain_cols = lax.dynamic_slice_in_dim(chain, col_start, tok_j, 0)

time: 127 us -> 89.8 us (0.71)
  waiting for transfers between devices: 39.7 us -> 13.8 us
  between operations: 13.7 us -> 0.23 us
  blocking collectives: 26.8 us -> 33.3 us
  starting transfers between devices: 8.57 us -> 3.62 us
  local copies, waits for them, and re-layouts: 23.4 us -> 25.2 us
    all_to_all x2 -> x1, waiting for transfers between devices: 36.7 us -> 13.8 us  [shards(): lax.all_to_all(product, axes, split_axis=0, concat_axis=0, tiled=True)]
    slice x0 -> x3, local copies, waits for them, and re-layouts: none -> 9.96 us  [the longest x2 6.85 us: shards(): both[1]]
    unnamed x28 -> x10, local copies, waits for them, and re-layouts: 8.29 us -> 0.81 us
    convert_element_type x3 -> x4, local copies, waits for them, and re-layouts: 7.42 us -> 0.7 us  [the longest x1 0.21 us: shards(): (pair_mask * jax.nn.sigmoid(right_g) * right_p).astype(jnp.bfloat16)]
    all_to_all x2 -> x1, blocking collectives: 26.8 us -> 33.3 us  [shards(): both = lax.all_to_all(both, axes, split_axis=0, concat_axis=0, tiled=True)]
    reshape x2 -> x4, local copies, waits for them, and re-layouts: 3.39 us -> 9.59 us  [the longest x2 4.73 us: shards(): product.transpose(1, 3, 0, 2, 4).reshape(n_dev, own, tok_i * tok_j)]
    all_to_all x2 -> x1, starting transfers between devices: 8.53 us -> 3.62 us  [shards(): lax.all_to_all(product, axes, split_axis=0, concat_axis=0, tiled=True)]
    all_gather x1 -> x0, waiting for transfers between devices: 2.95 us -> none  [shards(): lax.all_gather(right_c, 'row', axis=1, tiled=True)]
  transfers between devices with their start and end apart: 3 -> 1, of which waited for: 3 -> 1; matrix products, arithmetic and copies ran while one was open for 7% -> 2% of each run, Pallas kernels for 0% -> 0%
where the time goes in v1:
time: 89.8 us; the launch traced here: 89.1 us
  blocking collectives  33.3 us (37%)
  local copies, waits for them, and re-layouts  25.2 us (28%)
  waiting for transfers between devices  13.8 us (15%)
  other arithmetic  7.49 us (8%)
  matrix products  5.49 us (6%)
  starting transfers between devices  3.62 us (4%)
    all_to_all x1, blocking collectives, shards(): both = lax.all_to_all(both, axes, split_axis=0, concat_axis=0, tiled=True)  33.3 us
    all_to_all x1, waiting for transfers between devices, shards(): lax.all_to_all(product, axes, split_axis=0, concat_axis=0, tiled=True)  13.8 us
    slice x2, local copies, waits for them, and re-layouts, shards(): both[1]  6.85 us
    reshape x2, local copies, waits for them, and re-layouts, shards(): product.transpose(1, 3, 0, 2, 4).reshape(n_dev, own, tok_i * tok_j)  4.73 us
    reshape x1, local copies, waits for them, and re-layouts, shards(): both.reshape(n_row, n_col, 2, own, tok_i, tok_j).transpose(2, 3, 0, 4, 1, 5)  4.45 us
    all_to_all x1, starting transfers between devices, shards(): lax.all_to_all(product, axes, split_axis=0, concat_axis=0, tiled=True)  3.62 us
    slice x1, local copies, waits for them, and re-layouts, shards(): both[0]  3.11 us
    reduce_sum x2, other arithmetic, channel_norm(): spread = jnp.mean(centred * centred, axis=axis, keepdims=True)  2.03 us
  transfers between devices with their start and end apart: 1, of which 1 were waited for; matrix products, arithmetic and copies ran while one was open for 2% of the time, Pallas kernels for 0%

profile of v1, /device:TPU:0, one launch (start us, length us, event | category | flops | bytes accessed | tf_op | source)
XLA Modules:
  0.0 89.1 jit_solution(8185367852065778922)
XLA Ops:
  0.0 0.0 copy-start
  0.0 0.7 convert_element_type.48
  0.7 0.1 dynamic_slice.14
  0.8 0.1 dynamic_slice.15
  0.8 0.1 broadcast_multiply_fusion
  0.9 0.1 mul.96
  1.0 1.4 %convert_reduce_fusion = f32[64,32]{1,0:T(8,128)S(1)} fusion(bf16[64,32,128]{2,1,0:T(8,128)(2,1)} %param.10), kind=kLoop, calls=%fused_computation.8 | loop fusion | flops 522240 | bytes 532480 | tf_op jit(solution)/shard_map/reduce_sum | solution.py:8
  2.4 1.7 %fusion.7 = f32[64,32]{1,0:T(8,128)S(1)} fusion(bf16[64,32,128]{2,1,0:T(8,128)(2,1)} %param.10, f32[64,32]{1,0:T(8,128)S(1)} %broadcast_multiply_fusion.1), kind=kLoop, calls=%fused_computation.12 | loop fusion | flops 1046528 | bytes 540672 | tf_op jit(solution)/shard_map/reduce_sum | solution.py:10
  4.1 1.6 %fusion.8 = bf16[64,32,128]{2,1,0:T(8,128)(2,1)S(1)} fusion(bf16[64,32,128]{2,1,0:T(8,128)(2,1)} %param.10, f32[64,32]{1,0:T(8,128)S(1)} %add_rsqrt_fusion, f32[64,32]{1,0:T(8,128)S(1)} %broadcast_multiply_fusion.1), kind=kLoop, calls=%fused_computation.13 | loop fusion | flops 1048576 | bytes 1064960 | tf_op jit(solution)/shard_map/convert_element_type | solution.py:24
  5.8 0.0 copy-start.1
  5.8 0.8 copy-done.1
  6.5 1.5 %fusion.21 = f32[2048,512]{1,0:T(8,128)S(1)} fusion(bf16[2048,128]{1,0:T(8,128)(2,1)S(1)} %bitcast.30, bf16[128,128]{1,0:T(8,128)(2,1)} %param.16, bf16[128,128]{1,0:T(8,128)(2,1)} %param.15, bf16[128,128]{1,0:T(8,128)(2,1)} %param.14, bf16[128,128]{1,0:T(8,128)(2,1)} %param.13), kind=kOutput, calls=%fused_computation.34 | convolution fusion | flops 268959744 | bytes 4849664 | tf_op jit(solution)/shard_map/dot_general | solution.py:27
  8.0 0.6 fusion.14
  8.6 0.2 copy.45
  8.8 0.2 stack.10
  9.0 0.2 copy.42
  9.3 0.2 stack.9
  9.5 0.7 maximum_bitcast_fusion
  10.2 0.6 copy.46
  10.8 33.3 %all_to_all.10 = bf16[32,2,4,2048]{3,2,1,0:T(4,128)(2,1)S(1)} all-to-all(bf16[32,2,4,2048]{3,2,1,0:T(4,128)(2,1)S(1)} %copy.46), channel_id=1, replica_groups=mesh['row'=4,'col'=8] {'row','col'}, dimensions={0} | all-to-all | bytes 2097152 | tf_op jit(solution)/shard_map/all_to_all | solution.py:41
  44.2 0.6 copy.47
  44.7 4.5 %reshape.96 = bf16[4,8,2,4,64,32]{5,4,1,0,3,2:T(8,128)(2,1)} reshape(bf16[32,2,4,2048]{3,0,2,1:T(8,128)(2,1)S(1)} %copy.47) | data formatting | bytes 2097152 | tf_op jit(solution)/shard_map/reshape | solution.py:42
  49.2 4.9 %fusion.30 = (bf16[1,4,4,64,8,32]{5,3,4,2,1,0:T(8,128)(2,1)S(1)}, bf16[1,4,4,64,8,32]{5,3,4,2,1,0:T(8,128)(2,1)}) fusion(bf16[2,4,4,64,8,32]{5,3,4,2,1,0:T(8,128)(2,1)} %bitcast.28), kind=kLoop, calls=%fused_computation.49 | loop fusion | bytes 2097152 | tf_op jit(solution)/shard_map/slice | solution.py:44
  54.1 3.1 %copy.48 = bf16[1,4,4,64,8,32]{3,2,5,4,1,0:T(4,128)(2,1)S(1)} copy(bf16[1,4,4,64,8,32]{5,3,4,2,1,0:T(8,128)(2,1)} %get-tuple-element.8) | data formatting | bytes 1048576 | tf_op jit(solution)/shard_map/slice | solution.py:44
  57.2 1.5 %squeeze.6 = bf16[4,256,256]{1,2,0:T(8,128)(2,1)} reshape(bf16[1,4,4,64,8,32]{3,2,5,4,1,0:T(4,128)(2,1)S(1)} %copy.48) | data formatting | bytes 1048576 | tf_op jit(solution)/shard_map/squeeze | solution.py:44
  58.7 1.9 %copy.49 = bf16[1,4,4,64,8,32]{3,2,5,4,1,0:T(4,128)(2,1)S(1)} copy(bf16[1,4,4,64,8,32]{5,3,4,2,1,0:T(8,128)(2,1)S(1)} %get-tuple-element.7) | data formatting | bytes 1048576 | tf_op jit(solution)/shard_map/slice | solution.py:44
  60.6 0.7 squeeze.7
  61.3 1.4 %convolution_convert_fusion = bf16[4,256,256]{2,1,0:T(8,128)(2,1)S(1)} fusion(bf16[4,256,256]{1,2,0:T(8,128)(2,1)} %squeeze.6, bf16[4,256,256]{1,2,0:T(8,128)(2,1)S(1)} %squeeze.7), kind=kOutput, calls=%fused_computation.9 | convolution fusion | flops 134479872 | bytes 1572864 | tf_op jit(solution)/shard_map/cki,ckj->cij/dot_general | solution.py:44
  62.7 0.2 copy.51
  62.9 0.0 copy-start.3
  62.9 0.0 copy-start.4
  62.9 0.4 reshape.97
  63.3 2.0 %copy.56 = bf16[4,8,4,64,32]{4,3,2,1,0:T(8,128)(2,1)S(1)} copy(bf16[4,8,4,64,32]{3,0,4,1,2:T(4,128)(2,1)S(1)} %bitcast.29) | data formatting | bytes 1048576 | tf_op jit(solution)/shard_map/reshape | solution.py:46
  65.3 2.8 %reshape.102 = bf16[32,4,2048]{2,1,0:T(4,128)(2,1)} reshape(bf16[4,8,4,64,32]{4,3,2,1,0:T(8,128)(2,1)S(1)} %copy.56) | data formatting | bytes 1048576 | tf_op jit(solution)/shard_map/reshape | solution.py:46
  68.1 3.6 %all-to-all-start.1 = ((bf16[32,4,2048]{2,1,0:T(4,128)(2,1)}), bf16[32,4,2048]{2,1,0:T(4,128)(2,1)S(1)}, u32[]{:S(2)}, u32[]{:S(2)}) async-start(bf16[32,4,2048]{2,1,0:T(4,128)(2,1)} %reshape.102), calls=%async_computation.1 | async-start | bytes 1048576 | tf_op jit(solution)/shard_map/all_to_all | solution.py:47
  71.7 0.0 copy-done.3
  71.7 0.0 copy-start.2
  71.7 0.1 dynamic_slice.12
  71.8 0.1 dynamic_slice.13
  71.9 0.1 compare_convert_fusion
  71.9 0.1 reshape.100
  72.0 0.0 copy-done
  72.0 0.0 copy-done.4
  72.0 1.5 %fusion.3 = f32[2048,128]{1,0:T(8,128)S(1)} fusion(bf16[2048,128]{1,0:T(8,128)(2,1)} %bitcast.31, bf16[128,128]{1,0:T(8,128)(2,1)S(1)} %copy-done, f32[128]{0:T(128)S(1)} %copy-done.4, f32[2048]{0:T(1024)S(1)} %reshape.100), kind=kOutput, calls=%fused_computation.5 | convolution fusion | flops 68419584 | bytes 1614336 | tf_op jit(solution)/shard_map/dot_general | solution.py:56
  73.5 13.8 %all-to-all-done.1 = bf16[32,4,2048]{2,1,0:T(4,128)(2,1)S(1)} async-done(((bf16[32,4,2048]{2,1,0:T(4,128)(2,1)}), bf16[32,4,2048]{2,1,0:T(4,128)(2,1)S(1)}, u32[]{:S(2)}, u32[]{:S(2)}) %all-to-all-start.1) | async-done | bytes 524320 | tf_op jit(solution)/shard_map/all_to_all | solution.py:47
  87.3 0.2 convert_reduce_fusion.1
  87.5 0.4 multiply_reduce_fusion
  87.9 0.1 reshape.101
  88.0 0.0 copy-done.2
  88.0 1.1 %fusion.4 = bf16[2048,128]{1,0:T(8,128)(2,1)} fusion(f32[2048,128]{1,0:T(8,128)S(1)} %fusion.3, bf16[128,128]{1,0:T(8,128)(2,1)S(1)} %copy-done.2, f32[128,2048]{1,0:T(8,128)S(1)} %reshape.101, f32[2048]{0:T(1024)S(1)} %add_rsqrt_fusion.1, f32[2048]{0:T(1024)S(1)} %broadcast_multiply_fusion.2), kind=kOutput, calls=%fused_computation.6 | convolution fusion | flops 68419584 | bytes 2670592 | tf_op jit(solution)/shard_map/cp,cd->pd/dot_general | solution.py:50
  (4 shorter events, 0.0 us)
Async XLA Ops:
  0.0 72.0 %copy-start = (bf16[128,128]{1,0:T(8,128)(2,1)S(1)}, bf16[128,128]{1,0:T(8,128)(2,1)}, u32[]{:S(2)}) copy-start(bf16[128,128]{1,0:T(8,128)(2,1)} %param.17) | copy-start | bytes 98308
  5.8 0.8 copy-start.1
  62.9 8.8 %copy-start.3 = (s32[256]{0:T(256)S(1)}, s32[256]{0:T(256)}, u32[]{:S(2)}) copy-start(s32[256]{0:T(256)} %param.12) | copy-start | bytes 3076
  62.9 9.1 %copy-start.4 = (f32[128]{0:T(128)S(1)}, f32[128]{0:T(128)}, u32[]{:S(2)}) copy-start(f32[128]{0:T(128)} %param.19) | copy-start | bytes 1540
  68.1 19.2 %all-to-all-start.1 = ((bf16[32,4,2048]{2,1,0:T(4,128)(2,1)}), bf16[32,4,2048]{2,1,0:T(4,128)(2,1)S(1)}, u32[]{:S(2)}, u32[]{:S(2)}) async-start(bf16[32,4,2048]{2,1,0:T(4,128)(2,1)} %reshape.102), calls=%async_computation.1 | async-start | bytes 1048576 | tf_op jit(solution)/shard_map/all_to_all | solution.py:47
  71.7 16.3 %copy-start.2 = (bf16[128,128]{1,0:T(8,128)(2,1)S(1)}, bf16[128,128]{1,0:T(8,128)(2,1)}, u32[]{:S(2)}) copy-start(bf16[128,128]{1,0:T(8,128)(2,1)} %param.18) | copy-start | bytes 98308

commit v2 on v1

v2 whole, which is shorter than its diff:
```python
import functools

import jax
import jax.numpy as jnp
from jax import lax
from jax.experimental import pallas as pl
from jax.experimental.pallas import tpu as pltpu
from jax.sharding import PartitionSpec as P

MESH = pl.DeviceIdType.MESH
F32 = jnp.float32
BF16 = jnp.bfloat16
LANES = 128


def swap_lane_groups(parts):
    count = len(parts)
    width = LANES // count
    parts = list(parts)
    group = lax.broadcasted_iota(jnp.int32, parts[0].shape, 1) // width
    step = 1
    while step < count:
        high = (group // step) % 2 == 1
        moved = list(parts)
        for g in range(count):
            if (g // step) % 2 == 0:
                low_part, high_part = parts[g], parts[g + step]
                moved[g] = jnp.where(high, pltpu.roll(high_part, step * width, 1), low_part)
                moved[g + step] = jnp.where(
                    high, high_part, pltpu.roll(low_part, LANES - step * width, 1)
                )
        parts = moved
        step *= 2
    return parts


def kernel(
    n_row,
    n_col,
    pair_ref,
    mask_ref,
    chain_ref,
    w_ap_ref,
    w_ag_ref,
    w_bp_ref,
    w_bg_ref,
    w_gate_ref,
    w_out_ref,
    bias_ref,
    out_ref,
    zn_ref,
    wt_ref,
    gate_ref,
    left_ref,
    right_ref,
    send_ref,
    recv_ref,
    a_ref,
    b_ref,
    x_ref,
    xsend_ref,
    xrecv_ref,
    mixed_ref,
    send_sem,
    recv_sem,
    xsend_sem,
    xrecv_sem,
):
    n_dev = n_row * n_col
    tok_i, tok_j, width = pair_ref.shape
    hidden = w_ap_ref.shape[1]
    own = hidden // n_dev
    groups = LANES // tok_j
    high = tok_i // groups
    tokens = mask_ref.shape[1]
    halves = n_col // groups
    row = lax.axis_index("row")
    col = lax.axis_index("col")
    me = row * n_col + col

    def peer(offset):
        other = lax.rem(me + offset, n_dev)
        return other, (lax.div(other, n_col), lax.rem(other, n_col))

    barrier = pltpu.get_barrier_semaphore()

    @pl.loop(1, n_dev)
    def _(offset):
        pl.semaphore_signal(barrier, inc=1, device_id=peer(offset)[1], device_id_type=MESH)

    def transposed(ref):
        return jnp.transpose(ref[...].astype(F32))

    mats = [transposed(ref).astype(BF16) for ref in (w_ap_ref, w_ag_ref, w_bp_ref, w_bg_ref)]
    for c in range(own):
        for m in range(4):
            wt_ref[c, m * n_dev : (m + 1) * n_dev, :] = mats[m][c * n_dev : (c + 1) * n_dev]

    lane = lax.broadcasted_iota(jnp.int32, (tokens, LANES), 1)
    token = lax.broadcasted_iota(jnp.int32, (tokens, LANES), 0)
    pick = jnp.where(token == col * tok_j + lane % tok_j, 1.0, 0.0).astype(BF16)
    token_row = lax.broadcasted_iota(jnp.int32, (high, tokens), 1)
    high_row = lax.broadcasted_iota(jnp.int32, (high, tokens), 0)
    group = lax.broadcasted_iota(jnp.int32, (high, LANES), 1) // tok_j

    def spread(ref):
        values = ref[...].astype(F32)
        wide = jnp.broadcast_to(values, (high, tokens))
        cols = jnp.dot(wide.astype(BF16), pick, preferred_element_type=F32)
        rows = jnp.zeros((high, LANES), F32)
        for g in range(groups):
            hit = token_row == row * tok_i + g * high + high_row
            value = jnp.sum(jnp.where(hit, wide, 0.0), axis=1, keepdims=True)
            rows = jnp.where(group == g, value, rows)
        return rows, cols

    mask_rows, mask_cols = spread(mask_ref)
    pair_mask = mask_rows * mask_cols
    chain_rows, chain_cols = spread(chain_ref)
    same = jnp.where(chain_rows == chain_cols, 1.0, 0.0)

    @pl.loop(0, high)
    def _(h):
        block = jnp.concatenate([pair_ref[g * high + h] for g in range(groups)], axis=0)
        z = jnp.transpose(block.astype(F32))
        z = z - jnp.mean(z, axis=0, keepdims=True)
        spread_z = jnp.mean(z * z, axis=0, keepdims=True)
        zn_ref[h] = (z * lax.rsqrt(spread_z + 1e-05)).astype(BF16)

    pl.semaphore_wait(barrier, n_dev - 1)

    for c in range(own):
        for h in range(high):
            y = jnp.dot(wt_ref[c], zn_ref[h], preferred_element_type=F32)
            m = pair_mask[h : h + 1, :]
            left = m * jax.nn.sigmoid(y[n_dev : 2 * n_dev]) * y[:n_dev]
            right = m * jax.nn.sigmoid(y[3 * n_dev :]) * y[2 * n_dev : 3 * n_dev]
            left_ref[pl.ds(h, n_dev, stride=high), :] = left
            right_ref[pl.ds(h, n_dev, stride=high), :] = right
        send_ref[c, :, 0] = left_ref[...].astype(BF16).reshape(n_dev, high, LANES)
        send_ref[c, :, 1] = right_ref[...].astype(BF16).reshape(n_dev, high, LANES)
        recv_ref[c, me] = send_ref[c, me]

        @pl.loop(1, n_dev)
        def _(offset):
            other, place = peer(offset)
            pltpu.make_async_remote_copy(
                src_ref=send_ref.at[c, other],
                dst_ref=recv_ref.at[c, me],
                send_sem=send_sem.at[c],
                recv_sem=recv_sem.at[c],
                device_id=place,
                device_id_type=MESH,
            ).start()

    def wait_all(ref, sem):
        part = ref.at[pl.ds(0, n_dev - 1)]
        pltpu.make_async_copy(part, part, sem).wait()

    w_gate = transposed(w_gate_ref).astype(BF16)
    w_out = transposed(w_out_ref).astype(BF16)
    bias = jnp.transpose(jnp.broadcast_to(bias_ref[...], (LANES, width)))
    for h in range(high):
        gate = jnp.dot(w_gate, zn_ref[h], preferred_element_type=F32) + same[h : h + 1, :] * bias
        gate_ref[h] = jax.nn.sigmoid(gate)

    for c in range(own):
        wait_all(recv_ref.at[c], recv_sem.at[c])
        for which, target in ((0, a_ref), (1, b_ref)):
            for r in range(n_row):
                for q in range(halves):
                    base = r * n_col + q * groups
                    parts = [recv_ref[c, base + g, which].astype(F32) for g in range(groups)]
                    for g, part in enumerate(swap_lane_groups(parts)):
                        start = r * tok_i + g * high
                        target[start : start + high, q * LANES : (q + 1) * LANES] = part.astype(
                            BF16
                        )
        x_ref[...] = lax.dot_general(
            a_ref[...], b_ref[...], (((0,), (0,)), ((), ())), preferred_element_type=F32
        )
        for r in range(n_row):
            for q in range(halves):
                parts = [
                    x_ref[
                        r * tok_i + g * high : r * tok_i + (g + 1) * high,
                        q * LANES : (q + 1) * LANES,
                    ]
                    for g in range(groups)
                ]
                for g, part in enumerate(swap_lane_groups(parts)):
                    xsend_ref[c, r * n_col + q * groups + g] = part.astype(BF16)
        xrecv_ref[c, me] = xsend_ref[c, me]

        @pl.loop(1, n_dev)
        def _(offset):
            other, place = peer(offset)
            pltpu.make_async_remote_copy(
                src_ref=xsend_ref.at[c, other],
                dst_ref=xrecv_ref.at[c, me],
                send_sem=xsend_sem.at[c],
                recv_sem=xrecv_sem.at[c],
                device_id=place,
                device_id_type=MESH,
            ).start()

    for c in range(own):
        wait_all(xrecv_ref.at[c], xrecv_sem.at[c])
        span = n_dev * high
        mixed_ref[c * span : (c + 1) * span, :] = (
            xrecv_ref[c].astype(F32).reshape(span, LANES)
        )

    for h in range(high):
        x = mixed_ref[pl.ds(h, hidden, stride=high), :]
        x = x - jnp.mean(x, axis=0, keepdims=True)
        spread_x = jnp.mean(x * x, axis=0, keepdims=True)
        xn = (x * lax.rsqrt(spread_x + 1e-05)).astype(BF16)
        value = jnp.dot(w_out, xn, preferred_element_type=F32) * gate_ref[h]
        value = jnp.transpose(value).astype(BF16)
        for g in range(groups):
            out_ref[g * high + h] = value[g * tok_j : (g + 1) * tok_j, :]

    for c in range(own):
        wait_all(send_ref.at[c], send_sem.at[c])
        wait_all(xsend_ref.at[c], xsend_sem.at[c])


def shards(n_row, n_col, pair, mask, chain, w_ap, w_ag, w_bp, w_bg, w_gate, w_out, chain_bias):
    tok_i, tok_j, width = pair.shape
    hidden = w_ap.shape[1]
    n_dev = n_row * n_col
    own = hidden // n_dev
    groups = LANES // tok_j
    high = tok_i // groups
    tokens = mask.shape[0]
    vmem = pl.BlockSpec(memory_space=pltpu.VMEM)
    return pl.pallas_call(
        functools.partial(kernel, n_row, n_col),
        out_shape=jax.ShapeDtypeStruct(pair.shape, BF16),
        in_specs=[vmem] * 10,
        out_specs=vmem,
        scratch_shapes=[
            pltpu.VMEM((high, width, LANES), BF16),
            pltpu.VMEM((own, 4 * n_dev, width), BF16),
            pltpu.VMEM((high, width, LANES), F32),
            pltpu.VMEM((n_dev * high, LANES), F32),
            pltpu.VMEM((n_dev * high, LANES), F32),
            pltpu.VMEM((own, n_dev, 2, high, LANES), BF16),
            pltpu.VMEM((own, n_dev, 2, high, LANES), BF16),
            pltpu.VMEM((tokens, tokens), BF16),
            pltpu.VMEM((tokens, tokens), BF16),
            pltpu.VMEM((tokens, tokens), F32),
            pltpu.VMEM((own, n_dev, high, LANES), BF16),
            pltpu.VMEM((own, n_dev, high, LANES), BF16),
            pltpu.VMEM((hidden * high, LANES), F32),
            pltpu.SemaphoreType.DMA((own,)),
            pltpu.SemaphoreType.DMA((own,)),
            pltpu.SemaphoreType.DMA((own,)),
            pltpu.SemaphoreType.DMA((own,)),
        ],
        compiler_params=pltpu.CompilerParams(collective_id=0, has_side_effects=True),
        name="triangle",
    )(
        pair,
        mask.reshape(1, tokens),
        chain.reshape(1, tokens),
        w_ap,
        w_ag,
        w_bp,
        w_bg,
        w_gate,
        w_out,
        chain_bias.reshape(1, width),
    )


def solution(mesh):
    return jax.shard_map(
        functools.partial(shards, mesh.shape["row"], mesh.shape["col"]),
        mesh=mesh,
        in_specs=(P("row", "col", None), P(), P(), P(), P(), P(), P(), P(), P(), P()),
        out_specs=P("row", "col", None),
        check_vma=False,
    )
```

time: 89.8 us -> 47.5 us (0.53)
  Pallas kernels: 0 us -> 45.4 us
  blocking collectives: 33.3 us -> 0 us
  local copies, waits for them, and re-layouts: 25.2 us -> 1.87 us
  waiting for transfers between devices: 13.8 us -> 0 us
  other arithmetic: 7.49 us -> 0 us
  matrix products: 5.49 us -> 0 us
  starting transfers between devices: 3.62 us -> 0 us
    pallas_call x0 -> x1, Pallas kernels: none -> 45.4 us  [shards(): pl.pallas_call(functools.partial(kernel, n_row, n_col), out_shape=jax.Sha...]
    all_to_all x1 -> x0, blocking collectives: 33.3 us -> none  [shards(): both = lax.all_to_all(both, axes, split_axis=0, concat_axis=0, tiled=True)]
    all_to_all x1 -> x0, waiting for transfers between devices: 13.8 us -> none  [shards(): lax.all_to_all(product, axes, split_axis=0, concat_axis=0, tiled=True)]
    slice x3 -> x0, local copies, waits for them, and re-layouts: 9.96 us -> none  [the longest x2 6.85 us: shards(): both[1]]
    reshape x4 -> x0, local copies, waits for them, and re-layouts: 9.59 us -> none  [the longest x2 4.73 us: shards(): product.transpose(1, 3, 0, 2, 4).reshape(n_dev, own, tok_i * tok_j)]
    dot_general x4 -> x0, matrix products: 5.49 us -> none  [the longest x1 1.49 us: shards(): jnp.dot(flat, w_gate, preferred_element_type=jnp.float32)]
    reduce_sum x4 -> x0, other arithmetic: 3.65 us -> none  [the longest x2 2.03 us: channel_norm(): spread = jnp.mean(centred * centred, axis=axis, keepdims=True)]
    all_to_all x1 -> x0, starting transfers between devices: 3.62 us -> none  [shards(): lax.all_to_all(product, axes, split_axis=0, concat_axis=0, tiled=True)]
  transfers between devices with their start and end apart: 1 -> 0, of which waited for: 1 -> 0; matrix products, arithmetic and copies ran while one was open for 2% -> 0% of each run, Pallas kernels for 0% -> 0%
where the time goes in v2:
time: 47.5 us; the launch traced here: 47.3 us
  Pallas kernels  45.4 us (96%)
  local copies, waits for them, and re-layouts  1.87 us (4%)
    pallas_call x1, Pallas kernels, shards(): pl.pallas_call(functools.partial(kernel, n_row, n_col), out_shape=jax.Sha...  45.4 us
    unnamed x1, local copies, waits for them, and re-layouts  1.87 us

profile of v2, /device:TPU:0, one launch (start us, length us, event | category | flops | bytes accessed | tf_op | source)
XLA Modules:
  0.0 47.3 jit_solution(10011817213124587991)
XLA Ops:
  0.0 45.4 %triangle.1 = bf16[64,32,128]{2,1,0:T(8,128)(2,1)} custom-call(bf16[64,32,128]{2,1,0:T(8,128)(2,1)} %pair_ref.1, s32[1,256]{1,0:T(1,128)} %bitcast.3, s32[1,256]{1,0:T(1,128)} %bitcast.4, bf16[128,128]{1,0:T(8,128)(2,1)} %w_ap_ref.1, bf16[128,128]{1,0:T(8,128)(2,1)} %w_ag_ref.1, bf16[128,128]{1,0:T(8,128)(2,1)} %w_bp_ref.1, bf16[128,128]{1,0:T(8,128)(2,1)} %w_bg_ref.1, ...), custom_call_target="tpu_custom_call" | custom-call | tf_op jit(solution)/shard_map/triangle/pallas_call | solution.py:238
  45.4 1.9 %copy.12 = bf16[64,32,128]{2,1,0:T(8,128)(2,1)} copy(bf16[64,32,128]{2,1,0:T(8,128)(2,1)} %triangle.1) | data formatting | bytes 1048576

commit v3 on v2

--- a/solution.py
+++ b/solution.py
@@ -58,15 +58,21 @@
     a_ref,
     b_ref,
     x_ref,
+    keep_ref,
+    psend_ref,
+    precv_ref,
     xsend_ref,
     xrecv_ref,
     mixed_ref,
     send_sem,
     recv_sem,
+    psend_sem,
+    precv_sem,
     xsend_sem,
     xrecv_sem,
 ):
-    n_dev = n_row * n_col
+    half = n_row // 2
+    n_dev = half * n_col
     tok_i, tok_j, width = pair_ref.shape
     hidden = w_ap_ref.shape[1]
     own = hidden // n_dev
@@ -76,17 +82,22 @@
     halves = n_col // groups
     row = lax.axis_index("row")
     col = lax.axis_index("col")
-    me = row * n_col + col
+    base = lax.div(row, half) * half
+    far = n_row - half - base
+    me = (row - base) * n_col + col
+    partner = (lax.rem(row + half, n_row), col)
 
     def peer(offset):
         other = lax.rem(me + offset, n_dev)
-        return other, (lax.div(other, n_col), lax.rem(other, n_col))
+        return other, (base + lax.div(other, n_col), lax.rem(other, n_col))
 
     barrier = pltpu.get_barrier_semaphore()
 
     @pl.loop(1, n_dev)
     def _(offset):
         pl.semaphore_signal(barrier, inc=1, device_id=peer(offset)[1], device_id_type=MESH)
+
+    pl.semaphore_signal(barrier, inc=1, device_id=partner, device_id_type=MESH)
 
     def transposed(ref):
         return jnp.transpose(ref[...].astype(F32))
@@ -127,7 +138,7 @@
         spread_z = jnp.mean(z * z, axis=0, keepdims=True)
         zn_ref[h] = (z * lax.rsqrt(spread_z + 1e-05)).astype(BF16)
 
-    pl.semaphore_wait(barrier, n_dev - 1)
+    pl.semaphore_wait(barrier, n_dev)
 
     for c in range(own):
         for h in range(high):
@@ -164,13 +175,33 @@
         gate = jnp.dot(w_gate, zn_ref[h], preferred_element_type=F32) + same[h : h + 1, :] * bias
         gate_ref[h] = jax.nn.sigmoid(gate)
 
-    for c in range(own):
+    def partial_copy(c):
+        return pltpu.make_async_remote_copy(
+            src_ref=psend_ref.at[c],
+            dst_ref=precv_ref.at[c],
+            send_sem=psend_sem.at[c],
+            recv_sem=precv_sem.at[c],
+            device_id=partner,
+            device_id_type=MESH,
+        )
+
+    def token_rows(first, c, target):
+        for r in range(half):
+            for q in range(halves):
+                parts = []
+                for g in range(groups):
+                    start = pl.multiple_of((first + r) * tok_i + g * high, high)
+                    parts.append(x_ref[pl.ds(start, high), q * LANES : (q + 1) * LANES])
+                for g, part in enumerate(swap_lane_groups(parts)):
+                    target[c, r * n_col + q * groups + g] = part.astype(target.dtype)
+
+    def multiply(c):
         wait_all(recv_ref.at[c], recv_sem.at[c])
         for which, target in ((0, a_ref), (1, b_ref)):
-            for r in range(n_row):
+            for r in range(half):
                 for q in range(halves):
-                    base = r * n_col + q * groups
-                    parts = [recv_ref[c, base + g, which].astype(F32) for g in range(groups)]
+                    first = r * n_col + q * groups
+                    parts = [recv_ref[c, first + g, which].astype(F32) for g in range(groups)]
                     for g, part in enumerate(swap_lane_groups(parts)):
                         start = r * tok_i + g * high
                         target[start : start + high, q * LANES : (q + 1) * LANES] = part.astype(
@@ -179,17 +210,13 @@
         x_ref[...] = lax.dot_general(
             a_ref[...], b_ref[...], (((0,), (0,)), ((), ())), preferred_element_type=F32
         )
-        for r in range(n_row):
-            for q in range(halves):
-                parts = [
-                    x_ref[
-                        r * tok_i + g * high : r * tok_i + (g + 1) * high,
-                        q * LANES : (q + 1) * LANES,
-                    ]
-                    for g in range(groups)
-                ]
-                for g, part in enumerate(swap_lane_groups(parts)):
-                    xsend_ref[c, r * n_col + q * groups + g] = part.astype(BF16)
+        token_rows(far, c, psend_ref)
+        partial_copy(c).start()
+        token_rows(base, c, keep_ref)
+
+    def give_back(c):
+        partial_copy(c).wait_recv()
+        xsend_ref[c] = (keep_ref[c] + precv_ref[c].astype(F32)).astype(BF16)
         xrecv_ref[c, me] = xsend_ref[c, me]
 
         @pl.loop(1, n_dev)
@@ -204,6 +231,13 @@
                 device_id_type=MESH,
             ).start()
 
+    lag = max(own // 2, 1)
+    for c in range(own + lag):
+        if c < own:
+            multiply(c)
+        if c >= lag:
+            give_back(c - lag)
+
     for c in range(own):
         wait_all(xrecv_ref.at[c], xrecv_sem.at[c])
         span = n_dev * high
@@ -223,13 +257,15 @@
 
     for c in range(own):
         wait_all(send_ref.at[c], send_sem.at[c])
+        partial_copy(c).wait_send()
         wait_all(xsend_ref.at[c], xsend_sem.at[c])
 
 
 def shards(n_row, n_col, pair, mask, chain, w_ap, w_ag, w_bp, w_bg, w_gate, w_out, chain_bias):
     tok_i, tok_j, width = pair.shape
     hidden = w_ap.shape[1]
-    n_dev = n_row * n_col
+    half = n_row // 2
+    n_dev = half * n_col
     own = hidden // n_dev
     groups = LANES // tok_j
     high = tok_i // groups
@@ -248,12 +284,17 @@
             pltpu.VMEM((n_dev * high, LANES), F32),
             pltpu.VMEM((own, n_dev, 2, high, LANES), BF16),
             pltpu.VMEM((own, n_dev, 2, high, LANES), BF16),
-            pltpu.VMEM((tokens, tokens), BF16),
-            pltpu.VMEM((tokens, tokens), BF16),
+            pltpu.VMEM((half * tok_i, tokens), BF16),
+            pltpu.VMEM((half * tok_i, tokens), BF16),
             pltpu.VMEM((tokens, tokens), F32),
+            pltpu.VMEM((own, n_dev, high, LANES), F32),
+            pltpu.VMEM((own, n_dev, high, LANES), BF16),
+            pltpu.VMEM((own, n_dev, high, LANES), BF16),
             pltpu.VMEM((own, n_dev, high, LANES), BF16),
             pltpu.VMEM((own, n_dev, high, LANES), BF16),
             pltpu.VMEM((hidden * high, LANES), F32),
+            pltpu.SemaphoreType.DMA((own,)),
+            pltpu.SemaphoreType.DMA((own,)),
             pltpu.SemaphoreType.DMA((own,)),
             pltpu.SemaphoreType.DMA((own,)),
             pltpu.SemaphoreType.DMA((own,)),

time: 47.5 us -> 45.1 us (0.949)
  Pallas kernels: 45.4 us -> 43 us
    pallas_call x1, Pallas kernels: 45.4 us -> 43 us  [shards(): pl.pallas_call(functools.partial(kernel, n_row, n_col), out_shape=jax.Sha...]
where the time goes in v3:
time: 45.1 us; the launch traced here: 44.9 us
  Pallas kernels  43 us (95%)
  local copies, waits for them, and re-layouts  1.87 us (4%)
    pallas_call x1, Pallas kernels, shards(): pl.pallas_call(functools.partial(kernel, n_row, n_col), out_shape=jax.Sha...  43 us
    unnamed x1, local copies, waits for them, and re-layouts  1.87 us

profile of v3, /device:TPU:0, one launch (start us, length us, event | category | flops | bytes accessed | tf_op | source)
XLA Modules:
  0.0 44.9 jit_solution(1792463762228698775)
XLA Ops:
  0.0 43.0 %triangle.1 = bf16[64,32,128]{2,1,0:T(8,128)(2,1)} custom-call(bf16[64,32,128]{2,1,0:T(8,128)(2,1)} %pair_ref.1, s32[1,256]{1,0:T(1,128)} %bitcast.3, s32[1,256]{1,0:T(1,128)} %bitcast.4, bf16[128,128]{1,0:T(8,128)(2,1)} %w_ap_ref.1, bf16[128,128]{1,0:T(8,128)(2,1)} %w_ag_ref.1, bf16[128,128]{1,0:T(8,128)(2,1)} %w_bp_ref.1, bf16[128,128]{1,0:T(8,128)(2,1)} %w_bg_ref.1, ...), custom_call_target="tpu_custom_call" | custom-call | tf_op jit(solution)/shard_map/triangle/pallas_call | solution.py:274
  43.0 1.9 %copy.12 = bf16[64,32,128]{2,1,0:T(8,128)(2,1)} copy(bf16[64,32,128]{2,1,0:T(8,128)(2,1)} %triangle.1) | data formatting | bytes 1048576
